TPU v7x, 32 devices: a whole 2x2x4 slice. The times are simulated.
32 devices in a mesh: replica: 4 (over z), fsdp: 8 (over y, x, core).
Axes of the slice: x: 2, y: 2, z: 4, core: 2. Of those that a mesh axis runs over, the one named last changes fastest.
Arguments:
- states: bfloat16 [32, 256, 2048], P(('replica', 'fsdp'))
- cotangent: bfloat16 [32, 256, 512], P(('replica', 'fsdp')), may hold values from -6 to 6
- kv_weight: bfloat16 [2048, 512], P('fsdp'), may hold values from -0.125 to 0.125
- norm_gain: bfloat16 [2048], P('fsdp'), may hold values from -1.5 to 1.5
- prompt_len: int32 [32], P(('replica', 'fsdp')), may hold values from 1 to 255, as said below
- response_len: int32 [32], P(('replica', 'fsdp')), may hold values from 1 to 192
- reward_bucket: int32 [32], P(('replica', 'fsdp')), may hold values from 0 to 10, as said below
Outputs:
- key_values: bfloat16 [32, 256, 512], P(('replica', 'fsdp'))
- grad_weight: float32 [2048, 512], P('fsdp')
- grad_gain: float32 [2048], P('fsdp')
Inputs may be any that keep to these rules, and one draw needn't show every extreme that they name: prompt_len + response_len <= 256 for every rollout. `reward_bucket`: some rollout has level 0 and some has level 10.
All inputs are finite; a program needn't handle non-finite values.
Results may differ from a plain program's by a relative error of at most 0.005.
Values may be sent and summed in bfloat16 or wider, within the bound.
A program may use at most 64 MiB of HBM per device.

v0:
```python
import jax
import jax.numpy as jnp
from jax import lax
from jax.sharding import PartitionSpec as P

EPSILON = 1e-06
BLOCK_ROWS = 32


def normalize(states, gain_wide):
    widened = states.astype(jnp.float32)
    unit_rows = widened * lax.rsqrt(jnp.mean(widened * widened, axis=-1, keepdims=True) + EPSILON)
    return (unit_rows, (unit_rows * (1.0 + gain_wide)).astype(jnp.bfloat16))


def accumulate(unit_rows, normed, cotangent, coefficient, live_flag, weight_full):
    ordering = jnp.argsort(1 - live_flag, stable=True)
    unit_rows = jnp.take(unit_rows, ordering, axis=0)
    normed = jnp.take(normed, ordering, axis=0)
    cotangent = jnp.take(cotangent, ordering, axis=0)
    coefficient = jnp.take(coefficient, ordering, axis=0)
    row_total = normed.shape[0]
    width = normed.shape[1]
    feature_count = cotangent.shape[1]
    block_span = min(BLOCK_ROWS, row_total)
    block_count = (jnp.sum(live_flag) + block_span - 1) // block_span
    grad_shape = (width, feature_count)

    def one_block(step_index, totals):
        grad_weight, grad_gain = totals
        first_row = step_index * block_span
        unit_part = lax.dynamic_slice_in_dim(unit_rows, first_row, block_span, 0)
        normed_part = lax.dynamic_slice_in_dim(normed, first_row, block_span, 0)
        coef_part = lax.dynamic_slice_in_dim(coefficient, first_row, block_span, 0)
        cot_part = lax.dynamic_slice_in_dim(cotangent, first_row, block_span, 0)
        weighted = (coef_part[:, None] * cot_part.astype(jnp.float32)).astype(jnp.bfloat16)
        outer_part = jnp.einsum(
            "td,tk->dk", normed_part, weighted, preferred_element_type=jnp.float32
        )
        backward = jnp.einsum(
            "tk,dk->td", weighted, weight_full, preferred_element_type=jnp.float32
        )
        return (grad_weight + outer_part, grad_gain + jnp.sum(unit_part * backward, axis=0))

    start_totals = (jnp.zeros(grad_shape, jnp.float32), jnp.zeros((width,), jnp.float32))
    grad_weight, grad_gain = lax.fori_loop(0, block_count, one_block, start_totals)
    return (grad_weight, grad_gain)


def shards(states, cotangent, kv_weight, norm_gain, prompt_len, response_len, reward_bucket):
    weight_full, gain_full = (
        lax.all_gather(kv_weight, "fsdp", axis=0, tiled=True),
        lax.all_gather(norm_gain, "fsdp", axis=0, tiled=True),
    )
    gain_wide = gain_full.astype(jnp.float32)
    seq_states = states[0]
    seq_cotangent = cotangent[0]
    row_total = seq_states.shape[0]
    unit_rows, normed = normalize(seq_states, gain_wide)
    key_values = jnp.dot(normed, weight_full, preferred_element_type=jnp.float32).astype(
        jnp.bfloat16
    )[None]
    position = jnp.arange(row_total, dtype=jnp.int32)
    live_flag = ((position >= prompt_len[0]) & (position < prompt_len[0] + response_len[0])).astype(
        jnp.int32
    )
    reward_value = reward_bucket.astype(jnp.float32)
    reward_sum, square_sum, token_total = lax.psum(
        (reward_value, reward_value * reward_value, response_len.astype(jnp.float32)),
        ("replica", "fsdp"),
    )
    rollout_count = lax.axis_size("replica") * lax.axis_size("fsdp")
    average = reward_sum[0] / rollout_count
    variance = square_sum[0] / rollout_count - average * average
    grad_scale = lax.rsqrt(variance + EPSILON) * lax.rsqrt(token_total[0])
    coefficient = live_flag.astype(jnp.float32) * (reward_value[0] - average) * grad_scale
    work_unit, work_normed, work_cotangent, work_live = (
        unit_rows,
        normed,
        seq_cotangent,
        live_flag,
    )
    grad_weight, grad_gain = accumulate(
        work_unit, work_normed, work_cotangent, coefficient, work_live, weight_full
    )
    shares = (
        lax.psum_scatter(grad_weight, "fsdp", scatter_dimension=0, tiled=True),
        lax.psum_scatter(grad_gain, "fsdp", scatter_dimension=0, tiled=True),
    )
    weight_grad, gain_grad = lax.psum((shares[0], shares[1]), "replica")
    return (key_values, weight_grad, gain_grad)


def solution(mesh):
    placed = (
        P(("replica", "fsdp"), None, None),
        P(("replica", "fsdp"), None, None),
        P("fsdp", None),
        P("fsdp"),
        P(("replica", "fsdp")),
        P(("replica", "fsdp")),
        P(("replica", "fsdp")),
    )
    return jax.shard_map(
        shards,
        mesh=mesh,
        in_specs=placed,
        out_specs=(P(("replica", "fsdp"), None, None), P("fsdp", None), P("fsdp")),
        check_vma=False,
    )
```

profile of v0, /device:TPU:0, one launch (start us, length us, event | category | flops | bytes accessed | tf_op | source)
XLA Modules:
  0.0 230.7 jit_solution(2087397710774676146)
XLA Ops:
  7.2 0.0 copy-start
  7.2 0.0 all-gather.3.cloned.1.call-start
  7.2 0.7 all-gather.3.cloned.1.call-update
  7.9 0.0 reduce-scatter.2.cloned.1.call-start
  9.3 42.0 %all-reduce.1 = (f32[1]{0:T(128)}, f32[1]{0:T(128)}, f32[1]{0:T(128)}) all-reduce(f32[1]{0:T(128)S(6)} %mul.64, f32[1]{0:T(128)S(6)} %convert_element_type.40, f32[1]{0:T(128)S(6)} %convert_element_type.41), channel_id=1, replica_groups=mesh['replica'=4,'fsdp'=8] {'replica','fsdp'}, use_global_device_ids=true, to_apply=%region_4.0 | all-reduce | flops 3 | bytes 24 | tf_op jit(solution)/shard_map/psum | solution.py:68
  51.9 0.6 fusion.6
  53.2 0.7 reshape.74
  57.0 3.2 %sort.17 = (s32[256]{0:T(256)}, s32[256]{0:T(256)S(1)}) sort(s32[256]{0:T(256)S(1)} %get-tuple-element.81, s32[256]{0:T(256)S(1)} %iota.11), dimensions={0}, to_apply=%region_2.0 | sort | flops 2048 | bytes 4096 | tf_op jit(solution)/shard_map/jit(argsort)/sort | solution.py:17
  60.1 9.9 %all-gather = bf16[8,1,256]{2,1,0:T(2,128)(2,1)S(1)} all-gather(bf16[1,1,256]{2,1,0:T(2,128)(2,1)S(1)} %reshape.74), channel_id=1, replica_groups=mesh['replica'=4,'fsdp'=8] {'fsdp'}, dimensions={0}, use_global_device_ids=true | all-gather | bytes 4608 | tf_op jit(solution)/shard_map/all_gather | solution.py:53
  70.1 1.5 fusion.4
  71.6 1.5 convert_multiply_fusion
  73.2 2.4 %gather_fusion = bf16[256,2048]{1,0:T(8,128)(2,1)} fusion(bf16[256,2048]{1,0:T(8,128)(2,1)S(1)} %get-tuple-element.80, s32[1024]{0:T(1024)S(1)} %pad_clamp_fusion), kind=kCustom, calls=%fused_computation | custom fusion | bytes 2098176 | tf_op jit(solution)/shard_map/jit(_take)/gather | solution.py:19
  75.6 1.9 gather_fusion.1
  77.6 0.0 copy-done
  77.6 1.9 gather_fusion.2
  79.4 2.7 %gather_fusion.3 = f32[256,2048]{1,0:T(8,128)} fusion(f32[256,2048]{1,0:T(8,128)S(1)} %get-tuple-element.79, s32[1024]{0:T(1024)S(1)} %pad_clamp_fusion), kind=kCustom, calls=%fused_computation.3 | custom fusion | bytes 4195328 | tf_op jit(solution)/shard_map/jit(_take)/gather | solution.py:18
  82.1 0.0 copy-start.2
  82.2 1.9 broadcast_select_fusion.2
  84.1 2.5 %broadcast_select_fusion.1 = bf16[256,2048]{1,0:T(8,128)(2,1)} fusion(bf16[256,2048]{1,0:T(8,128)(2,1)} %gather_fusion, pred[256]{0:T(512)(128)(4,1)S(1)} %get-tuple-element.78), kind=kLoop, calls=%fused_computation.18 | loop fusion | flops 524288 | bytes 2097408 | tf_op jit(solution)/shard_map/jit(_take)/select_n | solution.py:19
  86.5 0.0 copy-done.2
  86.5 1.6 broadcast_select_fusion
  88.1 0.0 all-gather.3.cloned.1.call-done
  88.1 0.0 copy-start.1
  88.1 2.5 %broadcast_in_dim.49 = f32[2048,512]{1,0:T(8,128)} broadcast(f32[]{:T(128)} %constant.90.clone.1), dimensions={} | broadcast | bytes 4194308 | tf_op jit(solution)/shard_map/broadcast_in_dim | solution.py:45
  90.5 0.0 copy-done.1
  90.5 6.8 %while.12 = (s32[]{:T(128)}, f32[2048,512]{1,0:T(8,128)}, f32[2048]{0:T(1024)S(1)}, s32[]{:T(128)}, bf16[256,2048]{1,0:T(8,128)(2,1)}, /*index=5*/f32[256]{0:T(2...) while((s32[]{:T(128)}, f32[2048,512]{1,0:T(8,128)}, ...), condition=%wide.region_8.9_spmd, body=%wide.region_6.8_spmd.sunk | while | flops 135495680 | bytes 10980023 | solution.py:46
  90.5 0.1 dynamic_slice.27
  90.6 5.0 %convolution_add_fusion.2 = f32[2048,512]{1,0:T(8,128)} fusion(f32[2048,512]{1,0:T(8,128)} %get-tuple-element.153, bf16[256,2048]{1,0:T(8,128)(2,1)} %get-tuple-element.169, s32[]{:T(128)S(6)} %select_n.53, bf16[256,512]{1,0:T(8,128)(2,1)} %get-tuple-element.171, f32[32]{0:T(128)S(1)} %dynamic_slice.27), kind=kOutput, calls=%fused_computation.4.clone.1 | convolution fusion | flops 68206592 | bytes 8553600 | tf_op jit(solution)/shard_map/while/body/td,tk->dk/dot_general | solution.py:37
  95.6 1.7 fusion.16
  97.3 0.0 copy-start.3
  97.3 0.0 reduce-scatter.2.cloned.1.call-update
  97.3 0.0 all-reduce.4.cloned.1.call-start
  97.4 84.0 %reduce-scatter.2.cloned.1.call-done = f32[256,512]{1,0:T(8,128)} async-done(((f32[2048,512]{1,0:T(8,128)}), f32[256,512]{1,0:T(8,128)}) %reduce-scatter.2.cloned.1.call-update) | async-done | bytes 524304 | tf_op jit(solution)/shard_map/reduce_scatter | solution.py:87
  181.4 0.0 all-reduce.4.cloned.1.call-update
  181.4 0.0 copy-done.3
  181.4 0.6 dynamic-slice
  182.7 12.8 %all-reduce = f32[2048]{0:T(1024)S(1)} all-reduce(f32[2048]{0:T(1024)S(1)} %get-tuple-element.55), channel_id=3, replica_groups=mesh['replica'=4,'fsdp'=8] {'fsdp'}, use_global_device_ids=true, to_apply=%region_11.12.clone | all-reduce | flops 2048 | bytes 16384
  195.5 0.1 dynamic-slice.1
  195.6 12.6 %psum.39 = f32[256]{0:T(256)} all-reduce(f32[256]{0:T(256)S(1)} %dynamic-slice.1), channel_id=1, replica_groups=mesh['replica'=4,'fsdp'=8] {'replica'}, use_global_device_ids=true, to_apply=%region_12.13 | all-reduce | flops 256 | bytes 2048 | tf_op jit(solution)/shard_map/psum | solution.py:90
  208.2 1.4 fusion.5
  209.6 12.8 %all-reduce.4.cloned.1.call-done = f32[256,512]{1,0:T(8,128)} async-done(((f32[256,512]{1,0:T(8,128)}), f32[256,512]{1,0:T(8,128)}) %all-reduce.4.cloned.1.call-update) | async-done | bytes 524304 | tf_op jit(solution)/shard_map/psum | solution.py:90
  222.3 1.9 copy.23
  (9 shorter events, 0.1 us)
Async XLA Ops:
  7.2 70.4 %copy-start = (bf16[1,256,512]{2,1,0:T(8,128)(2,1)S(1)}, bf16[1,256,512]{2,1,0:T(8,128)(2,1)}, u32[]{:S(2)}) copy-start(bf16[1,256,512]{2,1,0:T(8,128)(2,1)} %param.10) | copy-start | bytes 786436
  7.2 80.9 %all-gather.3.cloned.1.call-start = ((), (), s32[]{:S(2)}) async-start(), calls=%async_computation.1 | async-start | bytes 2359296 | tf_op jit(solution)/shard_map/all_gather | solution.py:52
  7.9 173.5 %reduce-scatter.2.cloned.1.call-start = ((), (), s32[]{:S(2)}) async-start(), calls=%async_computation.2 | async-start | bytes 4718592 | tf_op jit(solution)/shard_map/reduce_scatter | solution.py:87
  82.1 4.4 %copy-start.2 = (f32[256,2048]{1,0:T(8,128)S(1)}, f32[256,2048]{1,0:T(8,128)}, u32[]{:S(2)}) copy-start(f32[256,2048]{1,0:T(8,128)} %gather_fusion.3) | copy-start | bytes 6291460
  88.1 2.5 %copy-start.1 = (bf16[2048,512]{1,0:T(8,128)(2,1)S(1)}, bf16[2048,512]{1,0:T(8,128)(2,1)}, u32[]{:S(2)}) copy-start(bf16[2048,512]{1,0:T(8,128)(2,1)} %all-gather.3.cloned.1.call-done) | copy-start | bytes 6291460
  97.3 84.1 %copy-start.3 = (u32[32]{0:T(128)S(1)}, u32[32]{0:T(128)}, u32[]{:S(2)}) copy-start(u32[32]{0:T(128)} %constant.113) | copy-start | bytes 388
  97.3 125.0 %all-reduce.4.cloned.1.call-start = ((), (), s32[]{:S(2)}) async-start(), calls=%async_computation.3 | async-start | bytes 1048576 | tf_op jit(solution)/shard_map/psum | solution.py:90
Sparse Core Ops, SparseCore 0:
  9.9 30.6 all-gather.2
  97.5 83.8 reduce-scatter.1
  183.8 38.5 all-reduce.3
where the time goes:
time: 231 us
  waiting for transfers between devices  97.5 us (42%)
  blocking collectives  77.3 us (33%)
  between operations  20.2 us (9%)
  local copies, waits for them, and re-layouts  14.7 us (6%)
  other arithmetic  12.8 us (6%)
  matrix products  8.07 us (3%)
    reduce_scatter x1, waiting for transfers between devices, shards(): lax.psum_scatter(grad_weight, 'fsdp', scatter_dimension=0, tiled=True)  84 us
    psum x1, blocking collectives, shards(): lax.psum((reward_value, reward_value * reward_value, response_len.astype(...  42 us
    unnamed x1, blocking collectives  12.8 us
    psum x1, waiting for transfers between devices, shards(): weight_grad, gain_grad = lax.psum((shares[0], shares[1]), 'replica')  12.8 us
    psum x1, blocking collectives, shards(): weight_grad, gain_grad = lax.psum((shares[0], shares[1]), 'replica')  12.6 us
    all_gather x1, blocking collectives, shards(): lax.all_gather(norm_gain, 'fsdp', axis=0, tiled=True)  9.94 us
    dot_general x1, matrix products, one_block(): jnp.einsum('td,tk->dk', normed_part, weighted, preferred_element_type=jnp...  4.96 us
  transfers between devices with their start and end apart: 3, of which 2 were waited for; matrix products, arithmetic and copies ran while one was open for 11% of the time, Pallas kernels for 0%

commit v1 on v0

v1 whole, which is shorter than its diff:
```python
import functools

import jax
import jax.numpy as jnp
from jax import lax
from jax.experimental import pallas as pl
from jax.experimental.pallas import tpu as pltpu
from jax.sharding import PartitionSpec as P

EPSILON = 1e-06
MESH = pl.DeviceIdType.MESH
BF = jnp.bfloat16
F32 = jnp.float32
TILE = 256


def flip(me, mask):
    out = me
    bit = 0
    while mask >> bit:
        if (mask >> bit) & 1:
            own = lax.rem(lax.div(me, 1 << bit), 2)
            out = out + (1 - 2 * own) * (1 << bit)
        bit += 1
    return out


def offset_of(position, order):
    count = len(order)
    return sum(((position >> (count - 1 - i)) & 1) << order[i] for i in range(count))


def kernel(
    R, F, chunk_rows,
    states_hbm, cot_hbm, weight_hbm, gain_ref, prompt_ref, response_ref, reward_ref,
    kv_ref, gw_ref, gg_ref,
    states, cot, normed, live_cot, inverse, w_rel, w_nat, grad, sending, receiving,
    gain_rel, gain_nat, scal_out, scal_in, zscal, gvec, gg_out, gg_in, gg_row, zgg,
    own, chain_out, chain_in,
    load_sem, send_sem, recv_sem,
):
    r, f = lax.axis_index("replica"), lax.axis_index("fsdp")
    bits = F.bit_length() - 1
    rest = list(range(1, bits))
    orders = ([0] + rest if bits else [], [0] + rest[::-1] if bits else [])
    rows, half = w_rel.shape[2], w_rel.shape[3]
    seq, width = states.shape
    row_parts = rows // chunk_rows
    chunks = 2 * row_parts
    tiles = width // TILE
    counter = [2 * chunks]
    pending = []

    def remote(src, dst, device):
        index = counter[0]
        counter[0] += 1
        copy = pltpu.make_async_remote_copy(
            src_ref=src, dst_ref=dst, send_sem=send_sem.at[index], recv_sem=recv_sem.at[index],
            device_id=device, device_id_type=MESH,
        )
        copy.start()
        pending.append(copy)
        return copy

    def across(bit):
        return (r, flip(f, 1 << bit))

    w_loads = []
    for p in range(2):
        w_loads.append(
            pltpu.make_async_copy(
                weight_hbm.at[:, pl.ds(p * half, half)], w_rel.at[p, 0], load_sem.at[p]
            )
        )
    state_load = pltpu.make_async_copy(states_hbm.at[0], states, load_sem.at[2])
    cot_load = pltpu.make_async_copy(cot_hbm.at[0], cot, load_sem.at[3])
    for copy in w_loads + [state_load, cot_load]:
        copy.start()

    gain_rel[0] = gain_ref[...].astype(F32)
    lane = lax.broadcasted_iota(jnp.int32, (8, 128), 1)
    reward = reward_ref[0].astype(F32)
    tokens = response_ref[0].astype(F32)
    zero = jnp.zeros((8, 128), F32)
    scal = jnp.where(lane == 0, zero + reward, zero)
    scal = jnp.where(lane == 1, zero + reward * reward, scal)
    scal = jnp.where(lane == 2, zero + tokens, scal)

    @pl.when(r == 0)
    def _():
        chain_in[0] = jnp.zeros(chain_in.shape[1:], chain_in.dtype)

    @pl.when(r == R - 1)
    def _():
        chain_in[1] = jnp.zeros(chain_in.shape[1:], chain_in.dtype)

    barrier = pltpu.get_barrier_semaphore()
    for bit in range(bits):
        pl.semaphore_signal(barrier, inc=1, device_id=across(bit), device_id_type=MESH)
    for k in range(1, R):
        pl.semaphore_signal(barrier, inc=1, device_id=(lax.rem(r + k, R), f), device_id_type=MESH)
    pl.semaphore_wait(barrier, bits + R - 1)

    def small_send(step, scal):
        bit = orders[0][bits - 1 - step]
        held = 1 << step
        scal_out[step] = scal
        return (
            remote(gain_rel.at[pl.ds(0, held)], gain_rel.at[pl.ds(held, held)], across(bit)),
            remote(scal_out.at[step], scal_in.at[step], across(bit)),
        )

    def small_wait(step, scal, copies):
        for copy in copies:
            copy.wait_recv()
        return scal + scal_in[step]

    def weight_send(step):
        held = 1 << step
        return [
            remote(
                w_rel.at[p, pl.ds(0, held)], w_rel.at[p, pl.ds(held, held)],
                across(orders[p][bits - 1 - step]),
            )
            for p in range(2)
        ]

    small = small_send(0, scal) if bits else None
    for copy in w_loads:
        copy.wait()
    moving = weight_send(0) if bits else []
    state_load.wait()

    def square_tile(i, total):
        part = states[:, pl.ds(pl.multiple_of(i * TILE, TILE), TILE)].astype(F32)
        return total + jnp.sum(part * part, axis=1, keepdims=True)

    squares = lax.fori_loop(0, tiles, square_tile, jnp.zeros((seq, 1), F32))
    inverse[...] = lax.rsqrt(squares / width + EPSILON)
    cot_load.wait()
    position = lax.broadcasted_iota(jnp.int32, (seq, cot.shape[1]), 0)
    first = prompt_ref[0]
    alive = (position >= first) & (position < first + response_ref[0])
    live_cot[...] = jnp.where(alive, cot[...].astype(F32), 0.0).astype(BF)

    for step in range(bits):
        scal = small_wait(step, scal, small)
        if step + 1 < bits:
            small = small_send(step + 1, scal)
        if step == 0 and bits > 1:
            for copy in moving:
                copy.wait_recv()
            moving = weight_send(1)

    scal_out[bits] = scal
    zcopies = [
        remote(scal_out.at[bits], zscal.at[k - 1], (lax.rem(r + k, R), f)) for k in range(1, R)
    ]
    for q in range(F):
        gain_nat[flip(f, offset_of(q, orders[0]))] = gain_rel[q]
    for b in range(F):
        gvec[:, b * rows:(b + 1) * rows] = gain_nat[b]

    def grad_tile(i, carry):
        at = pl.ds(pl.multiple_of(i * TILE, TILE), TILE)
        unit = states[:, at].astype(F32) * inverse[...]
        part = (unit * (1.0 + gvec[:, at])).astype(BF)
        normed[:, at] = part
        grad[at, :] = lax.dot_general(
            part, live_cot[...], (((0,), (0,)), ((), ())), preferred_element_type=F32
        )
        return carry

    lax.fori_loop(0, tiles, grad_tile, 0)

    for copy in zcopies:
        copy.wait_recv()
    for k in range(R - 1):
        scal = scal + zscal[k]
    count = float(R * F)

    def pick(which):
        return jnp.sum(jnp.where(lane[0:1] == which, scal[0:1], 0.0), axis=1, keepdims=True)

    average = pick(0) / count
    variance = pick(1) / count - average * average
    coef = (reward - average) * (lax.rsqrt(variance + EPSILON) * lax.rsqrt(pick(2)))

    starts = [F - (F >> i) for i in range(bits + 1)]

    def partial(p, q, step):
        begin = pl.multiple_of(flip(f, offset_of(q, orders[p])) * rows, rows)
        value = grad[pl.ds(begin, rows), p * half:(p + 1) * half] * coef
        for i in range(step):
            value = value + receiving[p, starts[i] + q].astype(F32)
        return value

    def scatter_send(p, step):
        keep = F >> (step + 1)
        for q in range(keep):
            sending[p, starts[step] + q] = partial(p, keep + q, step).astype(BF)
        at = pl.ds(starts[step], keep)
        return remote(sending.at[p, at], receiving.at[p, at], across(orders[p][step]))

    shares = [scatter_send(p, 0) for p in range(2)] if bits else []
    if bits > 1:
        for p in range(2):
            shares[p].wait_recv()
            shares[p] = scatter_send(p, 1)
    for step in range(2, bits):
        for copy in moving:
            copy.wait_recv()
        moving = weight_send(step)
    for p in range(2):
        if bits:
            moving[p].wait_recv()
        for q in range(F):
            begin = pl.multiple_of(flip(f, offset_of(q, orders[p])) * rows, rows)
            w_nat[pl.ds(begin, rows), p * half:(p + 1) * half] = w_rel[p, q]

    def gain_tile(i, carry):
        at = pl.ds(pl.multiple_of(i * TILE, TILE), TILE)
        backward = lax.dot_general(
            live_cot[...], w_nat[at, :], (((1,), (1,)), ((), ())), preferred_element_type=F32
        )
        unit = states[:, at].astype(F32) * inverse[...]
        gvec[:, at] = jnp.sum(unit * backward, axis=0, keepdims=True) * coef
        return carry

    lax.fori_loop(0, tiles, gain_tile, 0)
    for b in range(F):
        gg_out[0, b] = gvec[:, b * rows:(b + 1) * rows]
    gains = remote(gg_out.at[0], gg_in.at[0], across(0)) if bits else None
    kv_ref[0] = jnp.dot(normed[...], w_nat[...], preferred_element_type=F32).astype(BF)

    def gains_next(step):
        gains.wait_recv()
        gg_out[step] = gg_out[step - 1] + gg_in[step - 1]
        if step < bits:
            return remote(gg_out.at[step], gg_in.at[step], across(step))
        return None

    for step in range(2, bits):
        for p in range(2):
            shares[p].wait_recv()
            shares[p] = scatter_send(p, step)
        gains = gains_next(step - 1)

    near = lax.div(2 * r, R)

    def relay(way, c):
        step = 1 - 2 * way
        before, after = r - step, r + step
        has_before = (before >= 0) & (before < R)
        has_after = (after >= 0) & (after < R)
        index = way * chunks + c
        copy = pltpu.make_async_remote_copy(
            src_ref=chain_out.at[way, c], dst_ref=chain_in.at[way, c],
            send_sem=send_sem.at[index], recv_sem=recv_sem.at[index],
            device_id=(lax.rem(after + R, R), f), device_id_type=MESH,
        )

        @pl.when(has_before)
        def _():
            copy.wait_recv()

        @pl.when(has_after)
        def _():
            chain_out[way, c] = (own[c] + chain_in[way, c].astype(F32)).astype(chain_out.dtype)
            copy.start()

        return has_after, copy

    sent = []
    for p in range(2):
        if bits:
            shares[p].wait_recv()
        value = partial(p, 0, bits)
        for k in range(row_parts):
            own[p * row_parts + k] = value[k * chunk_rows:(k + 1) * chunk_rows]
    lead = min(2, chunks)
    for c in range(lead):
        sent.append(relay(near, c))
    if bits > 1:
        gains = gains_next(bits - 1)
    for c in range(chunks):
        sent.append(relay(1 - near, c))
        if c == 0:
            if bits:
                gains_next(bits)
            gg_row[...] = gg_out[bits, f]
            zgains = [
                remote(gg_row, zgg.at[k - 1], (lax.rem(r + k, R), f)) for k in range(1, R)
            ]
        if c + lead < chunks:
            sent.append(relay(near, c + lead))
        p, k = c // row_parts, c % row_parts
        gw_ref[k * chunk_rows:(k + 1) * chunk_rows, p * half:(p + 1) * half] = (
            own[c] + chain_in[0, c].astype(F32) + chain_in[1, c].astype(F32)
        )
    total = gg_row[...]
    for k in range(R - 1):
        zgains[k].wait_recv()
        total = total + zgg[k]
    gg_ref[...] = total
    for copy in pending:
        copy.wait_send()
    for has_after, copy in sent:
        @pl.when(has_after)
        def _(copy=copy):
            copy.wait_send()


def shards(R, F, states, cotangent, kv_weight, norm_gain, prompt_len, response_len, reward_bucket):
    _, seq, width = states.shape
    rows, features = kv_weight.shape
    half = features // 2
    bits = F.bit_length() - 1
    chunk_rows = max(rows // 2, min(rows, 32))
    chunks = 2 * (rows // chunk_rows)
    wire = BF if R <= 4 else F32
    semaphores = 2 * chunks + 7 * bits + 2 * (R - 1)
    zs = max(R - 1, 1)
    bs = max(bits, 1)
    vmem = pl.BlockSpec(memory_space=pltpu.VMEM)
    smem = pl.BlockSpec(memory_space=pltpu.SMEM)
    hbm = pl.BlockSpec(memory_space=pl.ANY)
    key_values, grad_weight, grad_gain = pl.pallas_call(
        functools.partial(kernel, R, F, chunk_rows),
        out_shape=(
            jax.ShapeDtypeStruct((1, seq, features), BF),
            jax.ShapeDtypeStruct((rows, features), F32),
            jax.ShapeDtypeStruct((1, rows), F32),
        ),
        in_specs=[hbm, hbm, hbm, vmem, smem, smem, smem],
        out_specs=(vmem, vmem, vmem),
        scratch_shapes=[
            pltpu.VMEM((seq, width), BF),
            pltpu.VMEM((seq, features), BF),
            pltpu.VMEM((seq, width), BF),
            pltpu.VMEM((seq, features), BF),
            pltpu.VMEM((seq, 1), F32),
            pltpu.VMEM((2, F, rows, half), BF),
            pltpu.VMEM((width, features), BF),
            pltpu.VMEM((width, features), F32),
            pltpu.VMEM((2, F, rows, half), BF),
            pltpu.VMEM((2, F, rows, half), BF),
            pltpu.VMEM((F, 1, rows), F32),
            pltpu.VMEM((F, 1, rows), F32),
            pltpu.VMEM((bits + 1, 8, 128), F32),
            pltpu.VMEM((bs, 8, 128), F32),
            pltpu.VMEM((zs, 8, 128), F32),
            pltpu.VMEM((1, width), F32),
            pltpu.VMEM((bits + 1, F, 1, rows), F32),
            pltpu.VMEM((bs, F, 1, rows), F32),
            pltpu.VMEM((1, rows), F32),
            pltpu.VMEM((zs, 1, rows), F32),
            pltpu.VMEM((chunks, chunk_rows, half), F32),
            pltpu.VMEM((2, chunks, chunk_rows, half), wire),
            pltpu.VMEM((2, chunks, chunk_rows, half), wire),
            pltpu.SemaphoreType.DMA((4,)),
            pltpu.SemaphoreType.DMA((semaphores,)),
            pltpu.SemaphoreType.DMA((semaphores,)),
        ],
        compiler_params=pltpu.CompilerParams(
            collective_id=0, has_side_effects=True, vmem_limit_bytes=56 * 1024 * 1024
        ),
    )(states, cotangent, kv_weight, norm_gain.reshape(1, rows), prompt_len, response_len, reward_bucket)
    return key_values, grad_weight, grad_gain.reshape(rows)


def solution(mesh):
    placed = (
        P(("replica", "fsdp"), None, None),
        P(("replica", "fsdp"), None, None),
        P("fsdp", None),
        P("fsdp"),
        P(("replica", "fsdp")),
        P(("replica", "fsdp")),
        P(("replica", "fsdp")),
    )
    return jax.shard_map(
        functools.partial(shards, mesh.shape["replica"], mesh.shape["fsdp"]),
        mesh=mesh,
        in_specs=placed,
        out_specs=(P(("replica", "fsdp"), None, None), P("fsdp", None), P("fsdp")),
        check_vma=False,
    )
```

time: 231 us -> 63.4 us (0.27)
  waiting for transfers between devices: 97.5 us -> 0 us
  blocking collectives: 77.3 us -> 0 us
  Pallas kernels: 0 us -> 56.9 us
  between operations: 20.2 us -> 2.62 us
  other arithmetic: 12.8 us -> 0 us
  local copies, waits for them, and re-layouts: 14.7 us -> 3.66 us
  matrix products: 8.07 us -> 0 us
    reduce_scatter x1 -> x0, waiting for transfers between devices: 84 us -> none  [shards(): lax.psum_scatter(grad_weight, 'fsdp', scatter_dimension=0, tiled=True)]
    pallas_call x0 -> x1, Pallas kernels: none -> 56.9 us  [shards(): pl.pallas_call(functools.partial(kernel, R, F, chunk_rows), out_shape=(ja...]
    psum x2 -> x0, blocking collectives: 54.6 us -> none  [the longest x1 42 us: shards(): lax.psum((reward_value, reward_value * reward_value, response_len.astype(...]
    unnamed x1 -> x0, blocking collectives: 12.8 us -> none
    psum x1 -> x0, waiting for transfers between devices: 12.8 us -> none  [shards(): weight_grad, gain_grad = lax.psum((shares[0], shares[1]), 'replica')]
    all_gather x1 -> x0, blocking collectives: 9.94 us -> none  [shards(): lax.all_gather(norm_gain, 'fsdp', axis=0, tiled=True)]
    gather x4 -> x0, local copies, waits for them, and re-layouts: 8.93 us -> none  [the longest x1 2.71 us: accumulate(): unit_rows = jnp.take(unit_rows, ordering, axis=0)]
    dot_general x3 -> x0, matrix products: 8.07 us -> none  [the longest x1 4.96 us: one_block(): jnp.einsum('td,tk->dk', normed_part, weighted, preferred_element_type=jnp...]
  transfers between devices with their start and end apart: 3 -> 0, of which waited for: 2 -> 0; matrix products, arithmetic and copies ran while one was open for 11% -> 0% of each run, Pallas kernels for 0% -> 0%
where the time goes in v1:
time: 63.4 us; the launch traced here: 63.2 us
  Pallas kernels  56.9 us (90%)
  local copies, waits for them, and re-layouts  3.66 us (6%)
  between operations  2.62 us (4%)
    pallas_call x1, Pallas kernels, shards(): pl.pallas_call(functools.partial(kernel, R, F, chunk_rows), out_shape=(ja...  56.9 us
    unnamed x9, local copies, waits for them, and re-layouts  3.1 us

profile of v1, /device:TPU:0, one launch (start us, length us, event | category | flops | bytes accessed | tf_op | source)
XLA Modules:
  0.0 63.2 jit_solution(5352461577768995309)
XLA Ops:
  1.9 0.0 copy-start.2
  2.6 0.0 copy-done.2
  2.6 0.6 reshape.12.gain_ref
  3.2 56.9 %shard_map.94 = (bf16[1,256,512]{2,1,0:T(8,128)(2,1)}, f32[256,512]{1,0:T(8,128)}, f32[1,256]{1,0:T(1,128)}) custom-call(bf16[1,256,2048]{2,1,0:T(8,128)(2,1)} %states_hbm.1, bf16[1,256,512]{2,1,0:T(8,128)(2,1)} %cot_hbm.1, bf16[256,512]{1,0:T(8,128)(2,1)} %weight_hbm.1, bf16[1,256]{1,0:T(2,128)(2,1)} %reshape.12.gain_ref, s32[1]{0:T(128)S(6)} %copy.13.prompt_ref, ...), custom_call_target="tpu_custom_call" | custom-call | tf_op jit(solution)/shard_map/pallas_call | solution.py:328
  60.1 0.0 copy-start
  60.1 1.7 %copy.16 = bf16[1,256,512]{2,1,0:T(8,128)(2,1)} copy(bf16[1,256,512]{2,1,0:T(8,128)(2,1)} %get-tuple-element.12) | data formatting | bytes 524288
  61.8 0.0 copy-done
  61.8 0.0 copy-start.1
  61.8 0.8 %copy.17 = f32[256,512]{1,0:T(8,128)} copy(f32[256,512]{1,0:T(8,128)S(1)} %copy-done) | data formatting | bytes 1048576
  62.6 0.0 copy-done.1
  62.6 0.6 copy.18
Async XLA Ops:
  1.9 0.7 %copy-start.2 = (bf16[256]{0:T(256)(128)(2,1)S(1)}, bf16[256]{0:T(256)(128)(2,1)}, u32[]{:S(2)}) copy-start(bf16[256]{0:T(256)(128)(2,1)} %param.10) | copy-start | bytes 1540
  60.1 1.7 %copy-start = (f32[256,512]{1,0:T(8,128)S(1)}, f32[256,512]{1,0:T(8,128)}, u32[]{:S(2)}) copy-start(f32[256,512]{1,0:T(8,128)} %get-tuple-element.13) | copy-start | bytes 1572868
  61.8 0.8 %copy-start.1 = (f32[1,256]{1,0:T(1,128)S(1)}, f32[1,256]{1,0:T(1,128)}, u32[]{:S(2)}) copy-start(f32[1,256]{1,0:T(1,128)} %get-tuple-element.8) | copy-start | bytes 3076

commit v2 on v1

--- a/solution.py
+++ b/solution.py
@@ -278,7 +278,7 @@
         value = partial(p, 0, bits)
         for k in range(row_parts):
             own[p * row_parts + k] = value[k * chunk_rows:(k + 1) * chunk_rows]
-    lead = min(2, chunks)
+    lead = chunks
     for c in range(lead):
         sent.append(relay(near, c))
     if bits > 1:

time: 63.4 us -> 51.9 us (0.82)
  Pallas kernels: 56.9 us -> 45.4 us
    pallas_call x1, Pallas kernels: 56.9 us -> 45.4 us  [shards(): pl.pallas_call(functools.partial(kernel, R, F, chunk_rows), out_shape=(ja...]
where the time goes in v2:
time: 51.9 us; the launch traced here: 51.7 us
  Pallas kernels  45.4 us (87%)
  local copies, waits for them, and re-layouts  3.66 us (7%)
  between operations  2.62 us (5%)
    pallas_call x1, Pallas kernels, shards(): pl.pallas_call(functools.partial(kernel, R, F, chunk_rows), out_shape=(ja...  45.4 us
    unnamed x9, local copies, waits for them, and re-layouts  3.1 us

profile of v2, /device:TPU:0, one launch (start us, length us, event | category | flops | bytes accessed | tf_op | source)
XLA Modules:
  0.0 51.7 jit_solution(170428310721617491)
XLA Ops:
  1.9 0.0 copy-start.2
  2.6 0.0 copy-done.2
  2.6 0.6 %reshape.12.gain_ref = bf16[1,256]{1,0:T(2,128)(2,1)} reshape(bf16[256]{0:T(256)(128)(2,1)S(1)} %copy-done.2) | data formatting | bytes 1024 | tf_op jit(solution)/shard_map/reshape | solution.py:368
  3.2 45.4 %shard_map.94 = (bf16[1,256,512]{2,1,0:T(8,128)(2,1)}, f32[256,512]{1,0:T(8,128)}, f32[1,256]{1,0:T(1,128)}) custom-call(bf16[1,256,2048]{2,1,0:T(8,128)(2,1)} %states_hbm.1, bf16[1,256,512]{2,1,0:T(8,128)(2,1)} %cot_hbm.1, bf16[256,512]{1,0:T(8,128)(2,1)} %weight_hbm.1, bf16[1,256]{1,0:T(2,128)(2,1)} %reshape.12.gain_ref, s32[1]{0:T(128)S(6)} %copy.13.prompt_ref, ...), custom_call_target="tpu_custom_call" | custom-call | tf_op jit(solution)/shard_map/pallas_call | solution.py:328
  48.6 0.0 copy-start
  48.6 1.7 %copy.16 = bf16[1,256,512]{2,1,0:T(8,128)(2,1)} copy(bf16[1,256,512]{2,1,0:T(8,128)(2,1)} %get-tuple-element.12) | data formatting | bytes 524288
  50.3 0.0 copy-done
  50.3 0.0 copy-start.1
  50.3 0.8 %copy.17 = f32[256,512]{1,0:T(8,128)} copy(f32[256,512]{1,0:T(8,128)S(1)} %copy-done) | data formatting | bytes 1048576
  51.1 0.0 copy-done.1
  51.1 0.6 %copy.18 = f32[256]{0:T(256)} copy(f32[256]{0:T(256)S(1)} %bitcast.1) | data formatting | bytes 2048
Async XLA Ops:
  1.9 0.7 %copy-start.2 = (bf16[256]{0:T(256)(128)(2,1)S(1)}, bf16[256]{0:T(256)(128)(2,1)}, u32[]{:S(2)}) copy-start(bf16[256]{0:T(256)(128)(2,1)} %param.10) | copy-start | bytes 1540
  48.6 1.7 %copy-start = (f32[256,512]{1,0:T(8,128)S(1)}, f32[256,512]{1,0:T(8,128)}, u32[]{:S(2)}) copy-start(f32[256,512]{1,0:T(8,128)} %get-tuple-element.13) | copy-start | bytes 1572868
  50.3 0.8 %copy-start.1 = (f32[1,256]{1,0:T(1,128)S(1)}, f32[1,256]{1,0:T(1,128)}, u32[]{:S(2)}) copy-start(f32[1,256]{1,0:T(1,128)} %get-tuple-element.8) | copy-start | bytes 3076
